TPU v7x, 128 devices: a whole 4x4x4 slice. The times are simulated.
128 devices in a mesh: row: 8 (over x, core), col: 16 (over z, y).
Axes of the slice: x: 4, y: 4, z: 4, core: 2. Of those that a mesh axis runs over, the one named last changes fastest.
Arguments:
- fock_matrix: float32 [4096, 4096], P('row', 'col'), as said below
- density: float32 [4096, 4096], P('row', 'col'), as said below
- basis_gram: float32 [4096, 4096], P('row', 'col'), as said below
- error_history: float32 [6, 4096, 4096], P(None, 'row', 'col'), as said below
- fock_history: float32 [6, 4096, 4096], P(None, 'row', 'col'), may hold values from -6 to 6
Outputs:
- fock_next: float32 [4096, 4096], P('row', 'col')
- error_new: float32 [4096, 4096], P('row', 'col')
- weights: float32 [7], replicated
Inputs may be any that keep to these rules, and one draw needn't show every extreme that they name: `fock_matrix`: symmetric. `density`: symmetric. `basis_gram`: symmetric. `error_history`: each of the 6 matrices is antisymmetric.
All inputs are finite; a program needn't handle non-finite values.
Results may differ from a plain program's by a relative error of at most 0.000098.
Values sent between devices are 32-bit elements; how exact they have to be, the bound alone decides.
A program may use at most 128 MiB of HBM per device.

v0:
```python
import jax
import jax.numpy as jnp
from jax import lax
from jax.sharding import Mesh
from jax.sharding import PartitionSpec as P

ROW = ("row_0", "row_1")
COL = ("col_0", "col_1")


def from_everyone(shard, axis):
    devices = lax.axis_size(axis)
    return lax.all_to_all(
        jnp.broadcast_to(shard[None], (devices, *shard.shape)), axis, 0, 0, tiled=True
    )


def laid_out(parts, dim):
    lengths = list(parts.shape[1:])
    lengths[dim] *= parts.shape[0]
    return jnp.moveaxis(parts, 0, dim).reshape(lengths)


def gathered_by_axis(shard, axes, dim):
    far, near = axes
    parts = from_everyone(from_everyone(shard, far), near)
    return laid_out(parts.swapaxes(0, 1).reshape(-1, *shard.shape), dim)


def from_partner(value, axis, stride):
    mask = 2**stride
    pairs = [(source, source ^ mask) for source in range(lax.axis_size(axis))]
    return lax.ppermute(value, axis, pairs)


def over_copies(shard, axis):
    return from_everyone(shard, axis).sum(axis=0)


def by_axis(shard, axes):
    far, near = axes
    nearer = over_copies(shard, near)
    return over_copies(nearer, far)


def body(fock_matrix, density, basis_gram, error_history, fock_history):
    highest = lax.Precision.HIGHEST
    row_index = lax.axis_index(ROW)
    col_index = lax.axis_index(COL)
    dens_rows = lax.all_gather(density, COL, axis=1, tiled=True)
    gram_cols = gathered_by_axis(basis_gram, ("row_0", "row_1"), 0)
    middle = jnp.dot(dens_rows, gram_cols, precision=highest, preferred_element_type=jnp.float32)
    fock_rows = lax.all_gather(fock_matrix, COL, axis=1, tiled=True)
    middle_cols = gathered_by_axis(middle, ("row_0", "row_1"), 0)
    product = jnp.dot(fock_rows, middle_cols, precision=highest, preferred_element_type=jnp.float32)
    block_cols = product.shape[1]
    own_bit = col_index % 2
    upper_half = product[:block_cols]
    lower_half = product[block_cols:]
    keep_half = jnp.where(own_bit == 0, upper_half, lower_half)
    send_half = jnp.where(own_bit == 0, lower_half, upper_half)
    partner_half = from_partner(send_half, COL, 0)
    moving = jnp.where(
        own_bit == 0,
        jnp.concatenate([keep_half, partner_half], axis=1),
        jnp.concatenate([partner_half, keep_half], axis=1),
    )
    row_bits = lax.axis_size(ROW).bit_length() - 1
    for level in range(row_bits):
        row_bit = row_index // 2**level % 2
        col_bit = col_index // 2 ** (level + 1) % 2
        passing = from_partner(moving, ROW, level)
        arrived = from_partner(passing, COL, level + 1)
        moving = jnp.where(row_bit != col_bit, arrived, moving)
    flipped = moving.T
    error_new = product - flipped
    stacked = jnp.concatenate([error_history, error_new[None]], axis=0)
    gram_local = jnp.einsum("kij,lij->kl", stacked, stacked, precision=highest)
    gram = by_axis(gram_local, ("row_0", ("row_1", "col_0", "col_1")))
    size = gram.shape[0]
    factor = jnp.linalg.cholesky(gram)
    forward = []
    for index in range(size):
        total = jnp.float32(1.0)
        for inner in range(index):
            total = total - factor[index, inner] * forward[inner]
        forward.append(total / factor[index, index])
    backward = [None] * size
    for index in range(size - 1, -1, -1):
        total = forward[index]
        for inner in range(index + 1, size):
            total = total - factor[inner, index] * backward[inner]
        backward[index] = total / factor[index, index]
    solved = jnp.stack(backward)
    weights = solved / jnp.sum(solved)
    history_count = fock_history.shape[0]
    fock_next = (
        jnp.einsum("k,kij->ij", weights[:history_count], fock_history, precision=highest)
        + weights[history_count] * fock_matrix
    )
    return (fock_next, error_new, weights)


def solution(mesh):
    split = Mesh(mesh.devices.reshape(4, 2, 4, 4), ("row_0", "row_1", "col_0", "col_1"))
    placed = (P(ROW, COL), P(ROW, COL), P(ROW, COL), P(None, ROW, COL), P(None, ROW, COL))
    return jax.shard_map(
        body,
        mesh=split,
        in_specs=placed,
        out_specs=(P(ROW, COL), P(ROW, COL), P()),
        check_vma=False,
    )
```

profile of v0, /device:TPU:0, one launch (start us, length us, event | category | flops | bytes accessed | tf_op | source)
XLA Modules:
  0.0 365.2 jit_solution(14596943696388433436)
XLA Ops:
  9.9 30.5 %all_to_all.30 = f32[4,512,256]{2,1,0:T(8,128)S(1)} all-to-all(f32[4,512,256]{2,1,0:T(8,128)S(1)} %broadcast_in_dim.15), channel_id=1, replica_groups=mesh['row_0'=4,'row_1'=2,'col_0'=4,'col_1'=4] {'row_0'}, dimensions={0} | all-to-all | bytes 4194304 | tf_op jit(solution)/shard_map/all_to_all | solution.py:13
  40.8 7.1 %all_to_all.31 = f32[2,4,512,256]{3,2,1,0:T(8,128)S(1)} all-to-all(f32[2,4,512,256]{3,2,1,0:T(8,128)S(1)} %broadcast_in_dim.16), channel_id=1, replica_groups=mesh['row_0'=4,'row_1'=2,'col_0'=4,'col_1'=4] {'row_1'}, dimensions={0} | all-to-all | bytes 8388608 | tf_op jit(solution)/shard_map/all_to_all | solution.py:13
  50.1 39.9 %all-gather.3.cloned.1.call-done = f32[512,4096]{1,0:T(8,128)} async-done(((f32[512,256]{1,0:T(8,128)}), f32[512,4096]{1,0:T(8,128)}) %all-gather.3.cloned.1.call-update) | async-done | bytes 8388624 | tf_op jit(solution)/shard_map/all_gather | solution.py:50
  90.0 9.8 %fusion.16 = f32[512,256]{1,0:T(8,128)S(1)} fusion(f32[512,4096]{1,0:T(8,128)} %all-gather.3.cloned.1.call-done, f32[4096,256]{1,0:T(8,128)} %bitcast.63), kind=kOutput, calls=%fused_computation.29 | convolution fusion | flops 6442450944 | bytes 13107200 | tf_op jit(solution)/shard_map/dot_general | solution.py:52
  101.3 4.5 %all-to-all-start.2 = ((f32[4,512,256]{2,1,0:T(8,128)}), f32[4,512,256]{2,1,0:T(8,128)}, u32[]{:S(2)}, u32[]{:S(2)}) async-start(f32[4,512,256]{2,1,0:T(8,128)} %broadcast_in_dim.17), calls=%async_computation.2 | async-start | bytes 4194304 | tf_op jit(solution)/shard_map/all_to_all | solution.py:13
  105.8 25.3 %all-to-all-done.2 = f32[4,512,256]{2,1,0:T(8,128)} async-done(((f32[4,512,256]{2,1,0:T(8,128)}), f32[4,512,256]{2,1,0:T(8,128)}, u32[]{:S(2)}, u32[]{:S(2)}) %all-to-all-start.2) | async-done | bytes 2097184 | tf_op jit(solution)/shard_map/all_to_all | solution.py:13
  133.1 7.1 %all_to_all.32 = f32[2,4,512,256]{3,2,1,0:T(8,128)S(1)} all-to-all(f32[2,4,512,256]{3,2,1,0:T(8,128)S(1)} %broadcast_in_dim.18), channel_id=1, replica_groups=mesh['row_0'=4,'row_1'=2,'col_0'=4,'col_1'=4] {'row_1'}, dimensions={0} | all-to-all | bytes 8388608 | tf_op jit(solution)/shard_map/all_to_all | solution.py:13
  140.2 2.2 copy.37
  142.5 26.3 %all-gather.5.cloned.1.call-done = f32[512,4096]{1,0:T(8,128)} async-done(((f32[512,256]{1,0:T(8,128)}), f32[512,4096]{1,0:T(8,128)}) %all-gather.5.cloned.1.call-update) | async-done | bytes 8388624 | tf_op jit(solution)/shard_map/all_gather | solution.py:53
  168.8 16.5 %convolution_bitcast_fusion = f32[512,256]{0,1:T(8,128)S(1)} fusion(f32[4096,256]{1,0:T(8,128)} %bitcast.62, f32[512,4096]{1,0:T(8,128)} %all-gather.5.cloned.1.call-done), kind=kOutput, calls=%fused_computation.6 | convolution fusion | flops 6442450944 | bytes 13107200 | tf_op jit(solution)/shard_map/dot_general | solution.py:55
  192.0 5.5 %collective-permute-done = f32[256,256]{1,0:T(8,128)S(1)} collective-permute-done((f32[256,256]{1,0:T(8,128)S(1)}, f32[256,256]{1,0:T(8,128)S(1)}, u32[]{:S(2)}, u32[]{:S(2)}) %collective-permute-start) | collective-permute-done | bytes 262176 | tf_op jit(solution)/shard_map/ppermute | solution.py:33
  202.5 13.7 %collective-permute-done.2 = f32[256,512]{1,0:T(8,128)} collective-permute-done((f32[256,512]{1,0:T(8,128)}, f32[256,512]{1,0:T(8,128)}, u32[]{:S(2)}, u32[]{:S(2)}) %collective-permute-start.2) | collective-permute-done | bytes 524320 | tf_op jit(solution)/shard_map/ppermute | solution.py:33
  219.6 11.7 %collective-permute-done.3 = f32[256,512]{1,0:T(8,128)} collective-permute-done((f32[256,512]{1,0:T(8,128)S(1)}, f32[256,512]{1,0:T(8,128)}, u32[]{:S(2)}, u32[]{:S(2)}) %collective-permute-start.3) | collective-permute-done | bytes 524320 | tf_op jit(solution)/shard_map/ppermute | solution.py:33
  232.5 11.4 %collective-permute-done.4 = f32[256,512]{1,0:T(8,128)} collective-permute-done((f32[256,512]{1,0:T(8,128)}, f32[256,512]{1,0:T(8,128)}, u32[]{:S(2)}, u32[]{:S(2)}) %collective-permute-start.4) | collective-permute-done | bytes 524320 | tf_op jit(solution)/shard_map/ppermute | solution.py:33
  245.8 3.0 collective-permute-start.5
  248.8 10.0 %collective-permute-done.5 = f32[256,512]{1,0:T(8,128)} collective-permute-done((f32[256,512]{1,0:T(8,128)S(1)}, f32[256,512]{1,0:T(8,128)}, u32[]{:S(2)}, u32[]{:S(2)}) %collective-permute-start.5) | collective-permute-done | bytes 524320 | tf_op jit(solution)/shard_map/ppermute | solution.py:33
  258.8 2.4 collective-permute-start.6
  261.2 5.7 %copy.40 = f32[6,512,256]{2,0,1:T(8,128)} copy(f32[6,512,256]{2,1,0:T(8,128)} %param.8) | data formatting | bytes 6291456 | tf_op args[3]
  267.0 4.2 %collective-permute-done.6 = f32[256,512]{1,0:T(8,128)} collective-permute-done((f32[256,512]{1,0:T(8,128)}, f32[256,512]{1,0:T(8,128)}, u32[]{:S(2)}, u32[]{:S(2)}) %collective-permute-start.6) | collective-permute-done | bytes 524320 | tf_op jit(solution)/shard_map/ppermute | solution.py:33
  275.2 13.4 %fusion.6 = f32[7,7]{1,0:T(8,128)S(1)} fusion(f32[1,512,256]{2,0,1:T(1,128)} %copy.41, f32[6,512,256]{2,0,1:T(8,128)} %copy.40), kind=kOutput, calls=%fused_computation.7 | convolution fusion | flops 77987840 | bytes 3670212 | tf_op jit(solution)/shard_map/kij,lij->kl/dot_general | solution.py:78
  288.7 12.8 %all_to_all.33 = f32[32,7,7]{2,1,0:T(8,128)S(1)} all-to-all(f32[32,7,7]{2,1,0:T(8,128)S(1)} %broadcast_in_dim.20), channel_id=1, replica_groups=mesh['row_0'=4,'row_1'=2,'col_0'=4,'col_1'=4] {'row_1','col_0','col_1'}, dimensions={0} | all-to-all | bytes 12544 | tf_op jit(solution)/shard_map/all_to_all | solution.py:13
  302.1 4.2 %all-to-all-start.5 = ((f32[4,7,7]{2,1,0:T(8,128)}), f32[4,7,7]{2,1,0:T(8,128)S(1)}, u32[]{:S(2)}, u32[]{:S(2)}) async-start(f32[4,7,7]{2,1,0:T(8,128)} %broadcast_in_dim.21), calls=%async_computation.5 | async-start | bytes 32768 | tf_op jit(solution)/shard_map/all_to_all | solution.py:13
  308.4 3.3 all-to-all-done.5
  351.7 5.2 %fusion.4 = f32[1,512,256]{2,0,1:T(1,128)S(1)} fusion(f32[6,512,256]{2,1,0:T(8,128)S(1)} %copy-done, f32[7]{0:T(128)S(1)} %broadcast_divide_fusion), kind=kOutput, calls=%fused_computation.4 | convolution fusion | flops 9437184 | bytes 3670044 | tf_op jit(solution)/shard_map/k,kij->ij/dot_general | solution.py:98
  (55 shorter events, 39.4 us)
Async XLA Ops:
  7.2 344.5 %copy-start = (f32[6,512,256]{2,1,0:T(8,128)S(1)}, f32[6,512,256]{2,1,0:T(8,128)}, u32[]{:S(2)}) copy-start(f32[6,512,256]{2,1,0:T(8,128)} %param.9) | copy-start | bytes 9437188
  7.2 82.8 %all-gather.3.cloned.1.call-start = ((), (), s32[]{:S(2)}) async-start(), calls=%async_computation.6 | async-start | bytes 8912896 | tf_op jit(solution)/shard_map/all_gather | solution.py:50
  7.9 160.9 %all-gather.5.cloned.1.call-start = ((), (), s32[]{:S(2)}) async-start(), calls=%async_computation.7 | async-start | bytes 8912896 | tf_op jit(solution)/shard_map/all_gather | solution.py:53
  101.3 29.8 %all-to-all-start.2 = ((f32[4,512,256]{2,1,0:T(8,128)}), f32[4,512,256]{2,1,0:T(8,128)}, u32[]{:S(2)}, u32[]{:S(2)}) async-start(f32[4,512,256]{2,1,0:T(8,128)} %broadcast_in_dim.17), calls=%async_computation.2 | async-start | bytes 4194304 | tf_op jit(solution)/shard_map/all_to_all | solution.py:13
  185.3 0.8 copy-start.1
  190.7 6.8 %collective-permute-start = (f32[256,256]{1,0:T(8,128)S(1)}, f32[256,256]{1,0:T(8,128)S(1)}, u32[]{:S(2)}, u32[]{:S(2)}) collective-permute-start(f32[256,256]{1,0:T(8,128)S(1)} %get-tuple-element.19), channel_id=1, source_target_pairs={{0,1},{1,0},{2,3},{3,2},{4,5},{5,4},{6,7},{7,6},{8,9},{9,8},{10,11... | collective-permute-start | bytes 786440 | tf_op jit(solution)/shard_map/ppermute | solution.py:33
  197.5 0.8 copy-start.5
  198.3 2.0 collective-permute-start.1
  200.4 15.8 %collective-permute-start.2 = (f32[256,512]{1,0:T(8,128)}, f32[256,512]{1,0:T(8,128)}, u32[]{:S(2)}, u32[]{:S(2)}) collective-permute-start(f32[256,512]{1,0:T(8,128)} %collective-permute-done.1), channel_id=1, source_target_pairs={{0,2},{1,3},{2,0},{3,1},{4,6},{5,7},{6,4},{7,5},{8,10},{9,11},{10,... | collective-permute-start | bytes 1572872 | tf_op jit(solution)/shard_map/ppermute | solution.py:33
  217.3 0.8 copy-start.4
  218.1 13.2 %collective-permute-start.3 = (f32[256,512]{1,0:T(8,128)S(1)}, f32[256,512]{1,0:T(8,128)}, u32[]{:S(2)}, u32[]{:S(2)}) collective-permute-start(f32[256,512]{1,0:T(8,128)S(1)} %broadcast_select_fusion), channel_id=1, source_target_pairs={{0,32},{16,48},{32,0},{48,16},{64,96},{80,112},{96,64},{112,80},{1... | collective-permute-start | bytes 1572872 | tf_op jit(solution)/shard_map/ppermute | solution.py:33
  231.3 12.6 %collective-permute-start.4 = (f32[256,512]{1,0:T(8,128)}, f32[256,512]{1,0:T(8,128)}, u32[]{:S(2)}, u32[]{:S(2)}) collective-permute-start(f32[256,512]{1,0:T(8,128)} %collective-permute-done.3), channel_id=1, source_target_pairs={{0,4},{1,5},{2,6},{3,7},{4,0},{5,1},{6,2},{7,3},{8,12},{9,13},{10,... | collective-permute-start | bytes 1572872 | tf_op jit(solution)/shard_map/ppermute | solution.py:33
  245.0 0.8 copy-start.2
  245.8 13.0 %collective-permute-start.5 = (f32[256,512]{1,0:T(8,128)S(1)}, f32[256,512]{1,0:T(8,128)}, u32[]{:S(2)}, u32[]{:S(2)}) collective-permute-start(f32[256,512]{1,0:T(8,128)S(1)} %broadcast_select_fusion.1), channel_id=1, source_target_pairs={{0,64},{16,80},{32,96},{48,112},{64,0},{80,16},{96,32},{112,48},{1... | collective-permute-start | bytes 1572872 | tf_op jit(solution)/shard_map/ppermute | solution.py:33
  258.8 12.4 %collective-permute-start.6 = (f32[256,512]{1,0:T(8,128)}, f32[256,512]{1,0:T(8,128)}, u32[]{:S(2)}, u32[]{:S(2)}) collective-permute-start(f32[256,512]{1,0:T(8,128)} %collective-permute-done.5), channel_id=1, source_target_pairs={{0,8},{1,9},{2,10},{3,11},{4,12},{5,13},{6,14},{7,15},{8,0},{9,1},... | collective-permute-start | bytes 1572872 | tf_op jit(solution)/shard_map/ppermute | solution.py:33
  302.1 9.6 %all-to-all-start.5 = ((f32[4,7,7]{2,1,0:T(8,128)}), f32[4,7,7]{2,1,0:T(8,128)S(1)}, u32[]{:S(2)}, u32[]{:S(2)}) async-start(f32[4,7,7]{2,1,0:T(8,128)} %broadcast_in_dim.21), calls=%async_computation.5 | async-start | bytes 32768 | tf_op jit(solution)/shard_map/all_to_all | solution.py:13
  351.1 5.8 %copy-start.3 = (f32[512,256]{1,0:T(8,128)S(1)}, f32[512,256]{1,0:T(8,128)}, u32[]{:S(2)}) copy-start(f32[512,256]{1,0:T(8,128)} %param.5) | copy-start | bytes 1572868
  351.1 7.3 %copy-start.6 = (f32[7]{0:T(128)}, f32[7]{0:T(128)S(1)}, u32[]{:S(2)}) copy-start(f32[7]{0:T(128)S(1)} %broadcast_divide_fusion) | copy-start | bytes 88
Sparse Core Ops, SparseCore 0:
  10.1 79.8 all-gather.2
  92.1 76.6 all-gather.4
where the time goes:
time: 367 us; the launch traced here: 365 us
  waiting for transfers between devices  155 us (42%)
  blocking collectives  57.6 us (16%)
  between operations  50 us (14%)
  matrix products  44.8 us (12%)
  local copies, waits for them, and re-layouts  28.9 us (8%)
  starting transfers between devices  20.3 us (6%)
  other arithmetic  8.92 us (2%)
    ppermute x7, waiting for transfers between devices, from_partner(): return lax.ppermute(value, axis, pairs)  58.6 us
    all_to_all x4, blocking collectives, from_everyone(): lax.all_to_all(jnp.broadcast_to(shard[None], (devices, *shard.shape)), ax...  57.6 us
    all_gather x1, waiting for transfers between devices, body(): dens_rows = lax.all_gather(density, COL, axis=1, tiled=True)  39.9 us
    all_to_all x2, waiting for transfers between devices, from_everyone(): lax.all_to_all(jnp.broadcast_to(shard[None], (devices, *shard.shape)), ax...  28.6 us
    all_gather x1, waiting for transfers between devices, body(): fock_rows = lax.all_gather(fock_matrix, COL, axis=1, tiled=True)  26.3 us
    dot_general x1, matrix products, body(): jnp.dot(fock_rows, middle_cols, precision=highest, preferred_element_type...  16.5 us
    unnamed x18, local copies, waits for them, and re-layouts  13.8 us
    dot_general x1, matrix products, body(): gram_local = jnp.einsum('kij,lij->kl', stacked, stacked, precision=highest)  13.4 us
  transfers between devices with their start and end apart: 11, of which 11 were waited for; matrix products, arithmetic and copies ran while one was open for 7% of the time, Pallas kernels for 0%

commit v1 on v0

--- a/solution.py
+++ b/solution.py
@@ -50,7 +50,8 @@
     dens_rows = lax.all_gather(density, COL, axis=1, tiled=True)
     gram_cols = gathered_by_axis(basis_gram, ("row_0", "row_1"), 0)
     middle = jnp.dot(dens_rows, gram_cols, precision=highest, preferred_element_type=jnp.float32)
-    fock_rows = lax.all_gather(fock_matrix, COL, axis=1, tiled=True)
+    sent = jnp.stack([fock_matrix] * lax.axis_size(COL))
+    fock_rows = jnp.concatenate(lax.all_to_all(sent, COL, 0, 0), axis=1)
     middle_cols = gathered_by_axis(middle, ("row_0", "row_1"), 0)
     product = jnp.dot(fock_rows, middle_cols, precision=highest, preferred_element_type=jnp.float32)
     block_cols = product.shape[1]

time: 367 us -> 467 us (1.27)
  waiting for transfers between devices: 155 us -> 254 us
  local copies, waits for them, and re-layouts: 28.9 us -> 37.6 us
  matrix products: 44.8 us -> 38.5 us
    all_to_all x0 -> x1, waiting for transfers between devices: none -> 121 us  [body(): fock_rows = jnp.concatenate(lax.all_to_all(sent, COL, 0, 0), axis=1)]
    all_gather x1 -> x0, waiting for transfers between devices: 26.3 us -> none  [body(): fock_rows = lax.all_gather(fock_matrix, COL, axis=1, tiled=True)]
    ppermute x7, waiting for transfers between devices: 58.6 us -> 65.6 us  [from_partner(): return lax.ppermute(value, axis, pairs)]
    ppermute x7, starting transfers between devices: 11.4 us -> 4.96 us  [from_partner(): return lax.ppermute(value, axis, pairs)]
    dot_general x1, matrix products: 16.5 us -> 10.2 us  [body(): jnp.dot(fock_rows, middle_cols, precision=highest, preferred_element_type...]
    all_to_all x0 -> x1, starting transfers between devices: none -> 5 us  [body(): fock_rows = jnp.concatenate(lax.all_to_all(sent, COL, 0, 0), axis=1)]
    unnamed x18 -> x21, local copies, waits for them, and re-layouts: 13.8 us -> 15.9 us
  transfers between devices with their start and end apart: 11 -> 11, of which waited for: 11 -> 11; matrix products, arithmetic and copies ran while one was open for 7% -> 4% of each run, Pallas kernels for 0% -> 0%
where the time goes in v1:
time: 467 us; the launch traced here: 465 us
  waiting for transfers between devices  254 us (54%)
  blocking collectives  58.6 us (13%)
  between operations  50 us (11%)
  matrix products  38.5 us (8%)
  local copies, waits for them, and re-layouts  37.6 us (8%)
  starting transfers between devices  17.9 us (4%)
  other arithmetic  8.92 us (2%)
    all_to_all x1, waiting for transfers between devices, body(): fock_rows = jnp.concatenate(lax.all_to_all(sent, COL, 0, 0), axis=1)  121 us
    ppermute x7, waiting for transfers between devices, from_partner(): return lax.ppermute(value, axis, pairs)  65.6 us
    all_to_all x4, blocking collectives, from_everyone(): lax.all_to_all(jnp.broadcast_to(shard[None], (devices, *shard.shape)), ax...  58.6 us
    all_gather x1, waiting for transfers between devices, body(): dens_rows = lax.all_gather(density, COL, axis=1, tiled=True)  40.4 us
    all_to_all x2, waiting for transfers between devices, from_everyone(): lax.all_to_all(jnp.broadcast_to(shard[None], (devices, *shard.shape)), ax...  26.3 us
    unnamed x21, local copies, waits for them, and re-layouts  15.9 us
    dot_general x1, matrix products, body(): gram_local = jnp.einsum('kij,lij->kl', stacked, stacked, precision=highest)  13.4 us
    dot_general x1, matrix products, body(): jnp.dot(fock_rows, middle_cols, precision=highest, preferred_element_type...  10.2 us
  transfers between devices with their start and end apart: 11, of which 11 were waited for; matrix products, arithmetic and copies ran while one was open for 4% of the time, Pallas kernels for 0%

profile of v1, /device:TPU:0, one launch (start us, length us, event | category | flops | bytes accessed | tf_op | source)
XLA Modules:
  0.0 465.5 jit_solution(4607002317429962753)
XLA Ops:
  9.3 30.5 %all_to_all.35 = f32[4,512,256]{2,1,0:T(8,128)S(1)} all-to-all(f32[4,512,256]{2,1,0:T(8,128)S(1)} %broadcast_in_dim.15), channel_id=1, replica_groups=mesh['row_0'=4,'row_1'=2,'col_0'=4,'col_1'=4] {'row_0'}, dimensions={0} | all-to-all | bytes 4194304 | tf_op jit(solution)/shard_map/all_to_all | solution.py:13
  40.2 7.1 %all_to_all.36 = f32[2,4,512,256]{3,2,1,0:T(8,128)S(1)} all-to-all(f32[2,4,512,256]{3,2,1,0:T(8,128)S(1)} %broadcast_in_dim.16), channel_id=1, replica_groups=mesh['row_0'=4,'row_1'=2,'col_0'=4,'col_1'=4] {'row_1'}, dimensions={0} | all-to-all | bytes 8388608 | tf_op jit(solution)/shard_map/all_to_all | solution.py:13
  49.6 40.4 %all-gather.2.cloned.1.call-done = f32[512,4096]{1,0:T(8,128)} async-done(((f32[512,256]{1,0:T(8,128)}), f32[512,4096]{1,0:T(8,128)}) %all-gather.2.cloned.1.call-update) | async-done | bytes 8388624 | tf_op jit(solution)/shard_map/all_gather | solution.py:50
  90.0 9.8 %fusion.16 = f32[512,256]{1,0:T(8,128)S(1)} fusion(f32[512,4096]{1,0:T(8,128)} %all-gather.2.cloned.1.call-done, f32[4096,256]{1,0:T(8,128)} %bitcast.66), kind=kOutput, calls=%fused_computation.29 | convolution fusion | flops 6442450944 | bytes 13107200 | tf_op jit(solution)/shard_map/dot_general | solution.py:52
  101.3 4.4 all-to-all-start.2
  107.8 23.3 %all-to-all-done.2 = f32[4,512,256]{2,1,0:T(8,128)} async-done(((f32[4,512,256]{2,1,0:T(8,128)}), f32[4,512,256]{2,1,0:T(8,128)}, u32[]{:S(2)}, u32[]{:S(2)}) %all-to-all-start.2) | async-done | bytes 2097184 | tf_op jit(solution)/shard_map/all_to_all | solution.py:13
  133.0 8.3 %all_to_all.37 = f32[2,4,512,256]{3,2,1,0:T(8,128)} all-to-all(f32[2,4,512,256]{3,2,1,0:T(8,128)S(1)} %broadcast_in_dim.18), channel_id=1, replica_groups=mesh['row_0'=4,'row_1'=2,'col_0'=4,'col_1'=4] {'row_1'}, dimensions={0} | all-to-all | bytes 8388608 | tf_op jit(solution)/shard_map/all_to_all | solution.py:13
  141.3 4.3 stack.18
  145.6 5.0 %all-to-all-start.4 = ((f32[16,512,256]{1,2,0:T(8,128)}), f32[16,512,256]{1,2,0:T(8,128)}, u32[]{:S(2)}, u32[]{:S(2)}) async-start(f32[16,512,256]{1,2,0:T(8,128)} %stack.18), calls=%async_computation.4 | async-start | bytes 16777216 | tf_op jit(solution)/shard_map/all_to_all | solution.py:54
  150.6 4.5 copy.40
  155.1 120.8 %all-to-all-done.4 = f32[16,512,256]{1,2,0:T(8,128)} async-done(((f32[16,512,256]{1,2,0:T(8,128)}), f32[16,512,256]{1,2,0:T(8,128)}, u32[]{:S(2)}, u32[]{:S(2)}) %all-to-all-start.4) | async-done | bytes 8388640 | tf_op jit(solution)/shard_map/all_to_all | solution.py:54
  275.9 10.2 %convolution_bitcast_fusion = f32[512,256]{0,1:T(8,128)S(1)} fusion(f32[4096,256]{1,0:T(8,128)} %bitcast.65, f32[512,4096]{0,1:T(8,128)} %bitcast.5), kind=kOutput, calls=%fused_computation.6 | convolution fusion | flops 6442450944 | bytes 13107200 | tf_op jit(solution)/shard_map/dot_general | solution.py:56
  291.7 7.2 %collective-permute-done = f32[256,256]{1,0:T(8,128)S(1)} collective-permute-done((f32[256,256]{1,0:T(8,128)S(1)}, f32[256,256]{1,0:T(8,128)S(1)}, u32[]{:S(2)}, u32[]{:S(2)}) %collective-permute-start) | collective-permute-done | bytes 262176 | tf_op jit(solution)/shard_map/ppermute | solution.py:33
  302.5 15.1 %collective-permute-done.2 = f32[256,512]{1,0:T(8,128)} collective-permute-done((f32[256,512]{1,0:T(8,128)}, f32[256,512]{1,0:T(8,128)}, u32[]{:S(2)}, u32[]{:S(2)}) %collective-permute-start.2) | collective-permute-done | bytes 524320 | tf_op jit(solution)/shard_map/ppermute | solution.py:33
  320.1 12.6 %collective-permute-done.3 = f32[256,512]{1,0:T(8,128)} collective-permute-done((f32[256,512]{1,0:T(8,128)S(1)}, f32[256,512]{1,0:T(8,128)}, u32[]{:S(2)}, u32[]{:S(2)}) %collective-permute-start.3) | collective-permute-done | bytes 524320 | tf_op jit(solution)/shard_map/ppermute | solution.py:33
  333.3 12.0 %collective-permute-done.4 = f32[256,512]{1,0:T(8,128)} collective-permute-done((f32[256,512]{1,0:T(8,128)}, f32[256,512]{1,0:T(8,128)}, u32[]{:S(2)}, u32[]{:S(2)}) %collective-permute-start.4) | collective-permute-done | bytes 524320 | tf_op jit(solution)/shard_map/ppermute | solution.py:33
  348.4 11.8 %collective-permute-done.5 = f32[256,512]{1,0:T(8,128)} collective-permute-done((f32[256,512]{1,0:T(8,128)S(1)}, f32[256,512]{1,0:T(8,128)}, u32[]{:S(2)}, u32[]{:S(2)}) %collective-permute-start.5) | collective-permute-done | bytes 524320 | tf_op jit(solution)/shard_map/ppermute | solution.py:33
  362.1 5.7 %copy.44 = f32[6,512,256]{2,0,1:T(8,128)} copy(f32[6,512,256]{2,1,0:T(8,128)} %param.8) | data formatting | bytes 6291456 | tf_op args[3]
  367.8 4.8 %collective-permute-done.6 = f32[256,512]{1,0:T(8,128)} collective-permute-done((f32[256,512]{1,0:T(8,128)}, f32[256,512]{1,0:T(8,128)}, u32[]{:S(2)}, u32[]{:S(2)}) %collective-permute-start.6) | collective-permute-done | bytes 524320 | tf_op jit(solution)/shard_map/ppermute | solution.py:33
  376.6 13.4 %fusion.6 = f32[7,7]{1,0:T(8,128)S(1)} fusion(f32[1,512,256]{2,0,1:T(1,128)} %copy.45, f32[6,512,256]{2,0,1:T(8,128)} %copy.44), kind=kOutput, calls=%fused_computation.7 | convolution fusion | flops 77987840 | bytes 3670212 | tf_op jit(solution)/shard_map/kij,lij->kl/dot_general | solution.py:79
  390.1 12.7 %all_to_all.38 = f32[32,7,7]{2,1,0:T(8,128)S(1)} all-to-all(f32[32,7,7]{2,1,0:T(8,128)S(1)} %broadcast_in_dim.20), channel_id=1, replica_groups=mesh['row_0'=4,'row_1'=2,'col_0'=4,'col_1'=4] {'row_1','col_0','col_1'}, dimensions={0} | all-to-all | bytes 12544 | tf_op jit(solution)/shard_map/all_to_all | solution.py:13
  403.4 3.5 all-to-all-start.6
  408.9 3.1 all-to-all-done.6
  452.0 5.2 %fusion.4 = f32[1,512,256]{2,0,1:T(1,128)S(1)} fusion(f32[6,512,256]{2,1,0:T(8,128)S(1)} %copy-done, f32[7]{0:T(128)S(1)} %broadcast_divide_fusion), kind=kOutput, calls=%fused_computation.4 | convolution fusion | flops 9437184 | bytes 3670044 | tf_op jit(solution)/shard_map/k,kij->ij/dot_general | solution.py:99
  (58 shorter events, 39.7 us)
Async XLA Ops:
  7.2 444.8 %copy-start = (f32[6,512,256]{2,1,0:T(8,128)S(1)}, f32[6,512,256]{2,1,0:T(8,128)}, u32[]{:S(2)}) copy-start(f32[6,512,256]{2,1,0:T(8,128)} %param.9) | copy-start | bytes 9437188
  7.2 82.8 %all-gather.2.cloned.1.call-start = ((), (), s32[]{:S(2)}) async-start(), calls=%async_computation.7 | async-start | bytes 8912896 | tf_op jit(solution)/shard_map/all_gather | solution.py:50
  101.3 29.8 %all-to-all-start.2 = ((f32[4,512,256]{2,1,0:T(8,128)}), f32[4,512,256]{2,1,0:T(8,128)}, u32[]{:S(2)}, u32[]{:S(2)}) async-start(f32[4,512,256]{2,1,0:T(8,128)} %broadcast_in_dim.17), calls=%async_computation.2 | async-start | bytes 4194304 | tf_op jit(solution)/shard_map/all_to_all | solution.py:13
  133.0 8.3 %copy-start.3 = (f32[512,256]{0,1:T(8,128)S(1)}, f32[512,256]{0,1:T(8,128)}, u32[]{:S(2)}) copy-start(f32[512,256]{0,1:T(8,128)} %copy.41) | copy-start | bytes 1572868
  145.6 130.3 %all-to-all-start.4 = ((f32[16,512,256]{1,2,0:T(8,128)}), f32[16,512,256]{1,2,0:T(8,128)}, u32[]{:S(2)}, u32[]{:S(2)}) async-start(f32[16,512,256]{1,2,0:T(8,128)} %stack.18), calls=%async_computation.4 | async-start | bytes 16777216 | tf_op jit(solution)/shard_map/all_to_all | solution.py:54
  286.1 0.8 copy-start.1
  291.6 7.3 %collective-permute-start = (f32[256,256]{1,0:T(8,128)S(1)}, f32[256,256]{1,0:T(8,128)S(1)}, u32[]{:S(2)}, u32[]{:S(2)}) collective-permute-start(f32[256,256]{1,0:T(8,128)S(1)} %get-tuple-element.19), channel_id=1, source_target_pairs={{0,1},{1,0},{2,3},{3,2},{4,5},{5,4},{6,7},{7,6},{8,9},{9,8},{10,11... | collective-permute-start | bytes 786440 | tf_op jit(solution)/shard_map/ppermute | solution.py:33
  298.9 0.8 copy-start.6
  299.7 2.0 collective-permute-start.1
  301.8 15.8 %collective-permute-start.2 = (f32[256,512]{1,0:T(8,128)}, f32[256,512]{1,0:T(8,128)}, u32[]{:S(2)}, u32[]{:S(2)}) collective-permute-start(f32[256,512]{1,0:T(8,128)} %collective-permute-done.1), channel_id=1, source_target_pairs={{0,2},{1,3},{2,0},{3,1},{4,6},{5,7},{6,4},{7,5},{8,10},{9,11},{10,... | collective-permute-start | bytes 1572872 | tf_op jit(solution)/shard_map/ppermute | solution.py:33
  318.7 0.8 copy-start.5
  319.5 13.2 %collective-permute-start.3 = (f32[256,512]{1,0:T(8,128)S(1)}, f32[256,512]{1,0:T(8,128)}, u32[]{:S(2)}, u32[]{:S(2)}) collective-permute-start(f32[256,512]{1,0:T(8,128)S(1)} %broadcast_select_fusion), channel_id=1, source_target_pairs={{0,32},{16,48},{32,0},{48,16},{64,96},{80,112},{96,64},{112,80},{1... | collective-permute-start | bytes 1572872 | tf_op jit(solution)/shard_map/ppermute | solution.py:33
  332.7 12.6 %collective-permute-start.4 = (f32[256,512]{1,0:T(8,128)}, f32[256,512]{1,0:T(8,128)}, u32[]{:S(2)}, u32[]{:S(2)}) collective-permute-start(f32[256,512]{1,0:T(8,128)} %collective-permute-done.3), channel_id=1, source_target_pairs={{0,4},{1,5},{2,6},{3,7},{4,0},{5,1},{6,2},{7,3},{8,12},{9,13},{10,... | collective-permute-start | bytes 1572872 | tf_op jit(solution)/shard_map/ppermute | solution.py:33
  346.4 0.8 copy-start.2
  347.2 13.0 %collective-permute-start.5 = (f32[256,512]{1,0:T(8,128)S(1)}, f32[256,512]{1,0:T(8,128)}, u32[]{:S(2)}, u32[]{:S(2)}) collective-permute-start(f32[256,512]{1,0:T(8,128)S(1)} %broadcast_select_fusion.1), channel_id=1, source_target_pairs={{0,64},{16,80},{32,96},{48,112},{64,0},{80,16},{96,32},{112,48},{1... | collective-permute-start | bytes 1572872 | tf_op jit(solution)/shard_map/ppermute | solution.py:33
  360.2 12.4 %collective-permute-start.6 = (f32[256,512]{1,0:T(8,128)}, f32[256,512]{1,0:T(8,128)}, u32[]{:S(2)}, u32[]{:S(2)}) collective-permute-start(f32[256,512]{1,0:T(8,128)} %collective-permute-done.5), channel_id=1, source_target_pairs={{0,8},{1,9},{2,10},{3,11},{4,12},{5,13},{6,14},{7,15},{8,0},{9,1},... | collective-permute-start | bytes 1572872 | tf_op jit(solution)/shard_map/ppermute | solution.py:33
  403.4 8.6 %all-to-all-start.6 = ((f32[4,7,7]{2,1,0:T(8,128)}), f32[4,7,7]{2,1,0:T(8,128)S(1)}, u32[]{:S(2)}, u32[]{:S(2)}) async-start(f32[4,7,7]{2,1,0:T(8,128)} %broadcast_in_dim.21), calls=%async_computation.6 | async-start | bytes 32768 | tf_op jit(solution)/shard_map/all_to_all | solution.py:13
  451.3 5.8 %copy-start.4 = (f32[512,256]{1,0:T(8,128)S(1)}, f32[512,256]{1,0:T(8,128)}, u32[]{:S(2)}) copy-start(f32[512,256]{1,0:T(8,128)} %param.5) | copy-start | bytes 1572868
  451.4 7.3 %copy-start.7 = (f32[7]{0:T(128)}, f32[7]{0:T(128)S(1)}, u32[]{:S(2)}) copy-start(f32[7]{0:T(128)S(1)} %broadcast_divide_fusion) | copy-start | bytes 88
Sparse Core Ops, SparseCore 0:
  10.1 79.8 all-gather.1
